TPU v7x, 32 devices: a whole 2x2x4 slice. The times are simulated.
32 devices in a mesh: runs: 2 (over y), gx: 4 (over z), gy: 2 (over x), gz: 2 (over core).
Axes of the slice: x: 2, y: 2, z: 4, core: 2. Of those that a mesh axis runs over, the one named last changes fastest.
Arguments:
- positions: float32 [3, 8, 4096], P(None, None, ('runs', 'gx', 'gy', 'gz')), parts along dimension 2, as said below
- velocities: float32 [3, 8, 4096], P(None, None, ('runs', 'gx', 'gy', 'gz')), parts along dimension 2, may hold values from -5 to 5
- send_list: int32 [5696], P(('runs', 'gx', 'gy', 'gz')), parts along dimension 0, may hold values from 0 to 127
- pair_list: int32 [2, 57344], P(None, ('runs', 'gx', 'gy', 'gz')), parts along dimension 1, may hold values from 0 to 306, as said below
- constraint_flags: int32 [7, 4096], P(None, ('runs', 'gx', 'gy', 'gz')), parts along dimension 1, may hold values 0 or 1
Outputs:
- final_positions: float32 [3, 8, 4096], P(None, None, ('runs', 'gx', 'gy', 'gz')), parts along dimension 2
- final_velocities: float32 [3, 8, 4096], P(None, None, ('runs', 'gx', 'gy', 'gz')), parts along dimension 2
- energies: float32 [6, 2], P('runs'), parts along dimension 0
There are 2 independent parts, one for each index of `runs`. A program takes and returns all parts, laid end to end along the dimension named above; each array names one. Nothing has to cross between parts.
Inputs may be any that keep to these rules, and one draw needn't show every extreme that they name: `pair_list`: each domain's 1792 slots name clusters of its extended set: 0 to 127 its own, then its received zone blocks in order; padding slots hold 306 in both rows; every cluster appears in a slot with itself; no unordered pair appears twice. `positions`: eight beads of a cluster lie in its cell of side 1, the cells of a domain filling a box of 1 by 8 by 16; neighbouring beads of a cluster are between 0.25 and 0.6 apart.
All inputs are finite; a program needn't handle non-finite values. No bound on the sum of `constraint_flags` on one device may be relied on, other than what follows from the above.
Results may differ from a plain program's by a relative error of at most 0.0003.
Values sent between devices are 32-bit elements; how exact they have to be, the bound alone decides.
A program may use at most 64 MiB of HBM per device.

v0:
```python
import jax
import jax.numpy as jnp
import numpy as np
from jax import lax
from jax.sharding import PartitionSpec as P

CX = 1
CY = 8
CZ = 16
ITERS = 3
NORDER = 4


time_step = 0.02
strength = 2.0
root_half = 0.7071067811865476
zone_list = ((1, 0, 0), (0, 1, 0), (0, 0, 1), (1, 1, 0), (1, 0, 1), (0, 1, 1), (1, 1, 1))


def from_behind(value, axis, by):
    count = lax.axis_size(axis)
    return lax.ppermute(value, axis, [(i, (i + by) % count) for i in range(count)])


def zone_sizes():
    return tuple(
        (
            (CX if direction[0] == 0 else 1)
            * (CY if direction[1] == 0 else 1)
            * (CZ if direction[2] == 0 else 1)
            for direction in zone_list
        )
    )


def split_blocks(packed, block_sizes):
    pieces = []
    position = 0
    for length in block_sizes:
        pieces.append(packed[:, :, position : position + length])
        position += length
    return pieces


def shell_offsets():
    block_sizes = zone_sizes()
    columns = []
    for number in range(7):
        direction = zone_list[number]
        column = np.array(
            [[direction[0] * CX], [direction[1] * CY], [direction[2] * CZ]], np.float32
        )
        columns.append(np.tile(column, (1, block_sizes[number])))
    return jnp.asarray(np.concatenate(columns, axis=1))[:, None, :]


def share_coords(coords, send_list):
    sizes_all = zone_sizes()
    outgoing = split_blocks(jnp.take(coords, send_list, axis=2), sizes_all)
    along_y = from_behind(
        jnp.concatenate([outgoing[1], outgoing[3], outgoing[5], outgoing[6]], axis=2), "gy", -1
    )
    got_y = split_blocks(along_y, [sizes_all[1], sizes_all[3], sizes_all[5], sizes_all[6]])
    along_x = from_behind(
        jnp.concatenate([outgoing[0], outgoing[4], got_y[1], got_y[3]], axis=2), "gx", -1
    )
    got_x = split_blocks(along_x, [sizes_all[0], sizes_all[4], sizes_all[3], sizes_all[6]])
    along_z = from_behind(
        jnp.concatenate([outgoing[2], got_x[1], got_y[2], got_x[3]], axis=2), "gz", -1
    )
    got_z = split_blocks(along_z, [sizes_all[2], sizes_all[4], sizes_all[5], sizes_all[6]])
    received = [got_x[0], got_y[0], got_z[0], got_x[2], got_z[1], got_z[2], got_z[3]]
    return jnp.concatenate(received, axis=2) + shell_offsets()


def return_forces(halo_forces):
    sizes_all = zone_sizes()
    outgoing = split_blocks(halo_forces, sizes_all)
    along_z = from_behind(
        jnp.concatenate([outgoing[2], outgoing[4], outgoing[5], outgoing[6]], axis=2), "gz", 1
    )
    got_z = split_blocks(along_z, [sizes_all[2], sizes_all[4], sizes_all[5], sizes_all[6]])
    along_x = from_behind(
        jnp.concatenate([outgoing[0], outgoing[3], got_z[1], got_z[3]], axis=2), "gx", 1
    )
    got_x = split_blocks(along_x, [sizes_all[0], sizes_all[3], sizes_all[4], sizes_all[6]])
    settled = [got_x[0], got_z[0], got_x[2]]
    pending = [got_x[1], got_z[2], got_x[3]]
    along_y = from_behind(
        jnp.concatenate([outgoing[1], pending[0], pending[1], pending[2]], axis=2), "gy", 1
    )
    got_y = split_blocks(along_y, [sizes_all[1], sizes_all[3], sizes_all[5], sizes_all[6]])
    return jnp.concatenate(
        [settled[0], got_y[0], settled[1], got_y[1], settled[2], got_y[2], got_y[3]], axis=2
    )


def pair_tables(pair_list, extended_count):
    rows = lax.broadcasted_iota(jnp.int32, (extended_count, pair_list.shape[1]), 0)
    first_table = (rows == pair_list[0][None, :]).astype(jnp.float32)
    second_table = (rows == pair_list[1][None, :]).astype(jnp.float32)
    return (first_table, second_table)


def domain_forces(extended, pair_list, tables):
    extended_count = extended.shape[2]
    slot_count = pair_list.shape[1]
    first_ids = pair_list[0]
    second_ids = pair_list[1]
    flat = extended.reshape(24, extended_count)
    first_coords = jnp.dot(flat, tables[0], precision=lax.Precision.HIGHEST).reshape(
        3, 8, slot_count
    )
    second_coords = jnp.dot(flat, tables[1], precision=lax.Precision.HIGHEST).reshape(
        3, 8, slot_count
    )
    separation = first_coords[:, :, None, :] - second_coords[:, None, :, :]
    scaled = jnp.sum(separation * separation, axis=0)
    intersect = jnp.maximum(1.0 - scaled, 0.0)
    bead_row = lax.broadcasted_iota(jnp.int32, (8, 8, 1), 0)
    bead_column = lax.broadcasted_iota(jnp.int32, (8, 8, 1), 1)
    self_pair = (first_ids == second_ids)[None, None, :]
    usable = (first_ids < extended_count - 1)[None, None, :]
    weight = (jnp.where(self_pair, bead_row < bead_column, True) & usable).astype(jnp.float32)
    energy = strength * jnp.sum(weight * intersect * intersect * intersect)
    magnitude = 6.0 * strength * weight * intersect * intersect
    pushing = magnitude[None] * separation
    on_first = jnp.sum(pushing, axis=2).reshape(24, slot_count)
    on_second = (-jnp.sum(pushing, axis=1)).reshape(24, slot_count)
    contract = (((1,), (1,)), ((), ()))
    forces = lax.dot_general(on_first, tables[0], contract, precision=lax.Precision.HIGHEST)
    forces = forces + lax.dot_general(
        on_second, tables[1], contract, precision=lax.Precision.HIGHEST
    )
    return (forces.reshape(3, 8, extended_count), energy)


def local_forces(coords, send_list, pair_list, tables):
    halo_coords = share_coords(coords, send_list)
    dummy_cluster = jnp.zeros((3, 8, 1), jnp.float32)
    extended = jnp.concatenate([coords, halo_coords, dummy_cluster], axis=2)
    forces, energy = domain_forces(extended, pair_list, tables)
    cluster_count = coords.shape[2]
    returned = return_forces(forces[:, :, cluster_count : cluster_count + send_list.shape[0]])
    home_forces = forces[:, :, :cluster_count].at[:, :, send_list].add(returned)
    return (home_forces, energy)


def link_vectors(coords):
    return coords[:, :-1, :] - coords[:, 1:, :]


def link_lengths(coords):
    vectors = link_vectors(coords)
    return jnp.sqrt(jnp.sum(vectors * vectors, axis=0))


def expand(coupling, source):
    coupling_down = jnp.pad(coupling, ((1, 0), (0, 0)))
    coupling_up = jnp.pad(coupling, ((0, 1), (0, 0)))
    series = source
    result = source
    for expansion in range(NORDER):
        series = (
            coupling_down * jnp.pad(series, ((1, 0), (0, 0)))[:-1]
            + coupling_up * jnp.pad(series, ((0, 1), (0, 0)))[1:]
        )
        result = result + series
    return result


def apply_links(coords, directions, solution):
    shifts = directions * (root_half * solution)[None]
    return (
        coords
        - jnp.pad(shifts, ((0, 0), (0, 1), (0, 0)))
        + jnp.pad(shifts, ((0, 0), (1, 0), (0, 0)))
    )


def constrain(previous, updated, rest_length, link_flags):
    old_vectors = link_vectors(previous)
    directions = (
        old_vectors / jnp.maximum(jnp.sqrt(jnp.sum(old_vectors * old_vectors, axis=0)), 0.2)[None]
    )
    coupling = (
        0.5
        * jnp.sum(directions[:, :-1] * directions[:, 1:], axis=0)
        * link_flags[:-1]
        * link_flags[1:]
    )
    projected = jnp.sum(directions * link_vectors(updated), axis=0)
    solution = expand(coupling, link_flags * root_half * (projected - rest_length))
    updated = apply_links(updated, directions, solution)
    vectors = link_vectors(updated)
    squared = jnp.sum(vectors * vectors, axis=0)
    target = jnp.sqrt(
        jnp.maximum(2.0 * rest_length * rest_length - squared, 0.25 * rest_length * rest_length)
    )
    solution = expand(coupling, link_flags * root_half * (rest_length - target))
    updated = apply_links(updated, directions, solution)
    return updated


def on_device(positions, velocities, send_list, pair_list, constraint_flags):
    link_flags = constraint_flags.astype(jnp.float32)
    rest_length = link_lengths(positions)
    bead_total = 8 * positions.shape[2] * lax.axis_size(("gx", "gy", "gz"))
    tables = pair_tables(pair_list, positions.shape[2] + send_list.shape[0] + 1)
    forces, potential = local_forces(positions, send_list, pair_list, tables)
    energy_rows = []
    for iteration in range(ITERS):
        half_speed = velocities + 0.5 * time_step * forces
        updated = constrain(positions, positions + time_step * half_speed, rest_length, link_flags)
        half_speed = (updated - positions) / time_step
        forces, potential = local_forces(updated, send_list, pair_list, tables)
        velocities = half_speed + 0.5 * time_step * forces
        positions = updated
        kinetic = 0.5 * jnp.sum(velocities * velocities)
        energy_rows.append(jnp.stack([potential, kinetic]))
    energies = jnp.stack(energy_rows)
    energies = lax.psum(energies, ("gx", "gy", "gz"))
    return (positions, velocities, energies / bead_total)


def solution(mesh):
    return jax.shard_map(
        on_device,
        mesh=mesh,
        in_specs=(
            P(None, None, ("runs", "gx", "gy", "gz")),
            P(None, None, ("runs", "gx", "gy", "gz")),
            P(("runs", "gx", "gy", "gz")),
            P(None, ("runs", "gx", "gy", "gz")),
            P(None, ("runs", "gx", "gy", "gz")),
        ),
        out_specs=(
            P(None, None, ("runs", "gx", "gy", "gz")),
            P(None, None, ("runs", "gx", "gy", "gz")),
            P("runs", None),
        ),
        check_vma=False,
    )
```

profile of v0, /device:TPU:0, one launch (start us, length us, event | category | flops | bytes accessed | tf_op | source)
XLA Modules:
  0.0 178.5 jit_solution(6793706241259081876)
XLA Ops:
  4.1 3.0 %collective-permute-start = (f32[3,8,34]{2,1,0:T(8,128)S(1)}, f32[3,8,34]{2,1,0:T(8,128)S(1)}, u32[]{:S(2)}, u32[]{:S(2)}) collective-permute-start(f32[3,8,34]{2,1,0:T(8,128)S(1)} %pad_maximum_fusion.8), channel_id=1, source_target_pairs={{0,2},{2,0},{1,3},{3,1},{4,6},{6,4},{5,7},{7,5},{8,10},{10,8},{9,1... | collective-permute-start | bytes 9800 | tf_op jit(solution)/shard_map/ppermute | solution.py:22
  7.2 1.5 collective-permute-done
  9.0 4.1 %collective-permute-start.1 = (f32[3,8,153]{2,1,0:T(8,128)S(1)}, f32[3,8,153]{2,1,0:T(8,128)S(1)}, u32[]{:S(2)}, u32[]{:S(2)}) collective-permute-start(f32[3,8,153]{2,1,0:T(8,128)S(1)} %pad_maximum_fusion), channel_id=1, source_target_pairs={{0,12},{4,0},{8,4},{12,8},{1,13},{5,1},{9,5},{13,9},{2,14},{6,2},{... | collective-permute-start | bytes 44072 | tf_op jit(solution)/shard_map/ppermute | solution.py:22
  13.2 1.5 collective-permute-done.1
  23.0 5.6 %collective-permute-done.4 = f32[3,8,153]{2,1,0:T(8,128)S(1)} collective-permute-done((f32[3,8,153]{2,1,0:T(8,128)S(1)}, f32[3,8,153]{2,1,0:T(8,128)S(1)}, u32[]{:S(2)}, u32[]{:S(2)}) %collective-permute-start.4) | collective-permute-done | bytes 14720 | tf_op jit(solution)/shard_map/ppermute | solution.py:22
  28.7 1.5 collective-permute-start.5
  30.5 2.0 %collective-permute-done.5 = f32[3,8,34]{2,1,0:T(8,128)S(1)} collective-permute-done((f32[3,8,34]{2,1,0:T(8,128)S(1)}, f32[3,8,34]{2,1,0:T(8,128)S(1)}, u32[]{:S(2)}, u32[]{:S(2)}) %collective-permute-start.5) | collective-permute-done | bytes 3296 | tf_op jit(solution)/shard_map/ppermute | solution.py:22
  32.9 7.2 %scatter_fusion = f32[3,8,128]{1,0,2:T(4,128)S(1)} fusion(f32[3,8,128]{1,0,2:T(4,128)S(1)} %copy.120, s32[178]{0:T(256)S(1)} %compare_select_fusion, f32[178,3,8]{2,1,0:T(4,128)S(1)} %copy.102), kind=kCustom, calls=%fused_computation.4 | custom fusion | flops 4272 | bytes 51976 | tf_op jit(solution)/shard_map/scatter-add | solution.py:145
  41.9 1.5 collective-permute-start.6
  43.4 2.1 %collective-permute-done.6 = f32[3,8,34]{2,1,0:T(8,128)S(1)} collective-permute-done((f32[3,8,34]{2,1,0:T(8,128)S(1)}, f32[3,8,34]{2,1,0:T(8,128)S(1)}, u32[]{:S(2)}, u32[]{:S(2)}) %collective-permute-start.6) | collective-permute-done | bytes 3296 | tf_op jit(solution)/shard_map/ppermute | solution.py:22
  45.8 2.0 %collective-permute-start.7 = (f32[3,8,153]{2,1,0:T(8,128)S(1)}, f32[3,8,153]{2,1,0:T(8,128)S(1)}, u32[]{:S(2)}, u32[]{:S(2)}) collective-permute-start(f32[3,8,153]{2,1,0:T(8,128)S(1)} %pad_maximum_fusion.2), channel_id=1, source_target_pairs={{0,12},{4,0},{8,4},{12,8},{1,13},{5,1},{9,5},{13,9},{2,14},{6,2},{... | collective-permute-start | bytes 44072 | tf_op jit(solution)/shard_map/ppermute | solution.py:22
  47.8 1.8 %collective-permute-done.7 = f32[3,8,153]{2,1,0:T(8,128)S(1)} collective-permute-done((f32[3,8,153]{2,1,0:T(8,128)S(1)}, f32[3,8,153]{2,1,0:T(8,128)S(1)}, u32[]{:S(2)}, u32[]{:S(2)}) %collective-permute-start.7) | collective-permute-done | bytes 14720 | tf_op jit(solution)/shard_map/ppermute | solution.py:22
  57.8 5.6 %collective-permute-done.10 = f32[3,8,153]{2,1,0:T(8,128)S(1)} collective-permute-done((f32[3,8,153]{2,1,0:T(8,128)S(1)}, f32[3,8,153]{2,1,0:T(8,128)S(1)}, u32[]{:S(2)}, u32[]{:S(2)}) %collective-permute-start.10) | collective-permute-done | bytes 14720 | tf_op jit(solution)/shard_map/ppermute | solution.py:22
  63.5 1.5 collective-permute-start.11
  65.3 2.0 %collective-permute-done.11 = f32[3,8,34]{2,1,0:T(8,128)S(1)} collective-permute-done((f32[3,8,34]{2,1,0:T(8,128)S(1)}, f32[3,8,34]{2,1,0:T(8,128)S(1)}, u32[]{:S(2)}, u32[]{:S(2)}) %collective-permute-start.11) | collective-permute-done | bytes 3296 | tf_op jit(solution)/shard_map/ppermute | solution.py:22
  67.7 7.2 %scatter_fusion.1 = f32[3,8,128]{1,0,2:T(4,128)S(1)} fusion(f32[3,8,128]{1,0,2:T(4,128)S(1)} %copy.121, s32[178]{0:T(256)S(1)} %compare_select_fusion, f32[178,3,8]{2,1,0:T(4,128)S(1)} %copy.107), kind=kCustom, calls=%fused_computation.5 | custom fusion | flops 4272 | bytes 51976 | tf_op jit(solution)/shard_map/scatter-add | solution.py:145
  76.7 1.5 collective-permute-start.12
  78.3 2.1 %collective-permute-done.12 = f32[3,8,34]{2,1,0:T(8,128)S(1)} collective-permute-done((f32[3,8,34]{2,1,0:T(8,128)S(1)}, f32[3,8,34]{2,1,0:T(8,128)S(1)}, u32[]{:S(2)}, u32[]{:S(2)}) %collective-permute-start.12) | collective-permute-done | bytes 3296 | tf_op jit(solution)/shard_map/ppermute | solution.py:22
  80.6 2.0 %collective-permute-start.13 = (f32[3,8,153]{2,1,0:T(8,128)S(1)}, f32[3,8,153]{2,1,0:T(8,128)S(1)}, u32[]{:S(2)}, u32[]{:S(2)}) collective-permute-start(f32[3,8,153]{2,1,0:T(8,128)S(1)} %pad_maximum_fusion.4), channel_id=1, source_target_pairs={{0,12},{4,0},{8,4},{12,8},{1,13},{5,1},{9,5},{13,9},{2,14},{6,2},{... | collective-permute-start | bytes 44072 | tf_op jit(solution)/shard_map/ppermute | solution.py:22
  82.7 1.8 %collective-permute-done.13 = f32[3,8,153]{2,1,0:T(8,128)S(1)} collective-permute-done((f32[3,8,153]{2,1,0:T(8,128)S(1)}, f32[3,8,153]{2,1,0:T(8,128)S(1)}, u32[]{:S(2)}, u32[]{:S(2)}) %collective-permute-start.13) | collective-permute-done | bytes 14720 | tf_op jit(solution)/shard_map/ppermute | solution.py:22
  92.4 5.6 %collective-permute-done.16 = f32[3,8,153]{2,1,0:T(8,128)S(1)} collective-permute-done((f32[3,8,153]{2,1,0:T(8,128)S(1)}, f32[3,8,153]{2,1,0:T(8,128)S(1)}, u32[]{:S(2)}, u32[]{:S(2)}) %collective-permute-start.16) | collective-permute-done | bytes 14720 | tf_op jit(solution)/shard_map/ppermute | solution.py:22
  98.2 1.5 collective-permute-start.17
  99.9 2.0 %collective-permute-done.17 = f32[3,8,34]{2,1,0:T(8,128)S(1)} collective-permute-done((f32[3,8,34]{2,1,0:T(8,128)S(1)}, f32[3,8,34]{2,1,0:T(8,128)S(1)}, u32[]{:S(2)}, u32[]{:S(2)}) %collective-permute-start.17) | collective-permute-done | bytes 3296 | tf_op jit(solution)/shard_map/ppermute | solution.py:22
  102.4 7.2 %scatter_fusion.2 = f32[3,8,128]{1,0,2:T(4,128)S(1)} fusion(f32[3,8,128]{1,0,2:T(4,128)S(1)} %copy.122, s32[178]{0:T(256)S(1)} %compare_select_fusion, f32[178,3,8]{2,1,0:T(4,128)S(1)} %copy.112), kind=kCustom, calls=%fused_computation.6 | custom fusion | flops 4272 | bytes 51976 | tf_op jit(solution)/shard_map/scatter-add | solution.py:145
  111.9 1.5 collective-permute-start.18
  113.5 2.1 %collective-permute-done.18 = f32[3,8,34]{2,1,0:T(8,128)S(1)} collective-permute-done((f32[3,8,34]{2,1,0:T(8,128)S(1)}, f32[3,8,34]{2,1,0:T(8,128)S(1)}, u32[]{:S(2)}, u32[]{:S(2)}) %collective-permute-start.18) | collective-permute-done | bytes 3296 | tf_op jit(solution)/shard_map/ppermute | solution.py:22
  115.9 2.2 %collective-permute-start.19 = (f32[3,8,153]{2,1,0:T(8,128)S(1)}, f32[3,8,153]{2,1,0:T(8,128)S(1)}, u32[]{:S(2)}, u32[]{:S(2)}) collective-permute-start(f32[3,8,153]{2,1,0:T(8,128)S(1)} %pad_maximum_fusion.6), channel_id=1, source_target_pairs={{0,12},{4,0},{8,4},{12,8},{1,13},{5,1},{9,5},{13,9},{2,14},{6,2},{... | collective-permute-start | bytes 44072 | tf_op jit(solution)/shard_map/ppermute | solution.py:22
  118.1 1.8 %collective-permute-done.19 = f32[3,8,153]{2,1,0:T(8,128)S(1)} collective-permute-done((f32[3,8,153]{2,1,0:T(8,128)S(1)}, f32[3,8,153]{2,1,0:T(8,128)S(1)}, u32[]{:S(2)}, u32[]{:S(2)}) %collective-permute-start.19) | collective-permute-done | bytes 14720 | tf_op jit(solution)/shard_map/ppermute | solution.py:22
  131.3 3.1 %collective-permute-done.22 = f32[3,8,153]{2,1,0:T(8,128)S(1)} collective-permute-done((f32[3,8,153]{2,1,0:T(8,128)S(1)}, f32[3,8,153]{2,1,0:T(8,128)S(1)}, u32[]{:S(2)}, u32[]{:S(2)}) %collective-permute-start.22) | collective-permute-done | bytes 14720 | tf_op jit(solution)/shard_map/ppermute | solution.py:22
  134.5 1.5 collective-permute-start.23
  138.7 7.2 %scatter_fusion.3 = f32[3,8,128]{1,0,2:T(4,128)S(1)} fusion(f32[3,8,128]{1,0,2:T(4,128)S(1)} %copy.123, s32[178]{0:T(256)S(1)} %compare_select_fusion, f32[178,3,8]{2,1,0:T(4,128)S(1)} %copy.117), kind=kCustom, calls=%fused_computation.7 | custom fusion | flops 4272 | bytes 51976 | tf_op jit(solution)/shard_map/scatter-add | solution.py:145
  147.9 29.9 %psum.7 = f32[3,2]{1,0:T(4,128)S(1)} all-reduce(f32[3,2]{1,0:T(4,128)S(1)} %pad_maximum_fusion.24), channel_id=1, replica_groups=mesh['runs'=2,'gx'=4,'gy'=2,'gz'=2] {'gx','gy','gz'}, use_global_device_ids=true, to_apply=%region_34.36 | all-reduce | flops 6 | bytes 48 | tf_op jit(solution)/shard_map/psum | solution.py:222
  (294 shorter events, 50.0 us)
Async XLA Ops:
  2.0 5.2 %copy-start.4 = (s32[2,1792]{1,0:T(2,128)S(1)}, s32[2,1792]{1,0:T(2,128)}, u32[]{:S(2)}) copy-start(s32[2,1792]{1,0:T(2,128)} %param.14) | copy-start | bytes 43012
  3.9 12.3 %copy-start.3 = (f32[3,178]{1,0:T(4,128)S(1)}, f32[3,178]{1,0:T(4,128)}, u32[]{:S(2)}) copy-start(f32[3,178]{1,0:T(4,128)} %constant.57.clone) | copy-start | bytes 6412
  3.9 12.3 %copy-start = (f32[3,8,128]{2,1,0:T(8,128)S(1)}, f32[3,8,128]{2,1,0:T(8,128)}, u32[]{:S(2)}) copy-start(f32[3,8,128]{2,1,0:T(8,128)} %param.11) | copy-start | bytes 36868
  4.1 4.6 %collective-permute-start = (f32[3,8,34]{2,1,0:T(8,128)S(1)}, f32[3,8,34]{2,1,0:T(8,128)S(1)}, u32[]{:S(2)}, u32[]{:S(2)}) collective-permute-start(f32[3,8,34]{2,1,0:T(8,128)S(1)} %pad_maximum_fusion.8), channel_id=1, source_target_pairs={{0,2},{2,0},{1,3},{3,1},{4,6},{6,4},{5,7},{7,5},{8,10},{10,8},{9,1... | collective-permute-start | bytes 9800 | tf_op jit(solution)/shard_map/ppermute | solution.py:22
  9.0 5.7 %collective-permute-start.1 = (f32[3,8,153]{2,1,0:T(8,128)S(1)}, f32[3,8,153]{2,1,0:T(8,128)S(1)}, u32[]{:S(2)}, u32[]{:S(2)}) collective-permute-start(f32[3,8,153]{2,1,0:T(8,128)S(1)} %pad_maximum_fusion), channel_id=1, source_target_pairs={{0,12},{4,0},{8,4},{12,8},{1,13},{5,1},{9,5},{13,9},{2,14},{6,2},{... | collective-permute-start | bytes 44072 | tf_op jit(solution)/shard_map/ppermute | solution.py:22
  14.8 1.2 collective-permute-start.2
  19.8 10.4 %copy-start.1 = (s32[7,128]{1,0:T(8,128)S(1)}, s32[7,128]{1,0:T(8,128)}, u32[]{:S(2)}) copy-start(s32[7,128]{1,0:T(8,128)} %param.15) | copy-start | bytes 10756
  21.2 1.2 collective-permute-start.3
  22.7 5.9 %collective-permute-start.4 = (f32[3,8,153]{2,1,0:T(8,128)S(1)}, f32[3,8,153]{2,1,0:T(8,128)S(1)}, u32[]{:S(2)}, u32[]{:S(2)}) collective-permute-start(f32[3,8,153]{2,1,0:T(8,128)S(1)} %pad_maximum_fusion.1), channel_id=1, source_target_pairs={{0,4},{4,8},{8,12},{12,0},{1,5},{5,9},{9,13},{13,1},{2,6},{6,10},{... | collective-permute-start | bytes 44072 | tf_op jit(solution)/shard_map/ppermute | solution.py:22
  28.7 3.7 %collective-permute-start.5 = (f32[3,8,34]{2,1,0:T(8,128)S(1)}, f32[3,8,34]{2,1,0:T(8,128)S(1)}, u32[]{:S(2)}, u32[]{:S(2)}) collective-permute-start(f32[3,8,34]{2,1,0:T(8,128)S(1)} %pad_maximum_fusion.11), channel_id=1, source_target_pairs={{0,2},{2,0},{1,3},{3,1},{4,6},{6,4},{5,7},{7,5},{8,10},{10,8},{9,1... | collective-permute-start | bytes 9800 | tf_op jit(solution)/shard_map/ppermute | solution.py:22
  30.5 9.7 %copy-start.5 = (f32[3,8,128]{2,1,0:T(8,128)S(1)}, f32[3,8,128]{2,1,0:T(8,128)}, u32[]{:S(2)}) copy-start(f32[3,8,128]{2,1,0:T(8,128)} %param.12) | copy-start | bytes 36868
  41.9 3.7 %collective-permute-start.6 = (f32[3,8,34]{2,1,0:T(8,128)S(1)}, f32[3,8,34]{2,1,0:T(8,128)S(1)}, u32[]{:S(2)}, u32[]{:S(2)}) collective-permute-start(f32[3,8,34]{2,1,0:T(8,128)S(1)} %pad_maximum_fusion.12), channel_id=1, source_target_pairs={{0,2},{2,0},{1,3},{3,1},{4,6},{6,4},{5,7},{7,5},{8,10},{10,8},{9,1... | collective-permute-start | bytes 9800 | tf_op jit(solution)/shard_map/ppermute | solution.py:22
  45.8 3.8 %collective-permute-start.7 = (f32[3,8,153]{2,1,0:T(8,128)S(1)}, f32[3,8,153]{2,1,0:T(8,128)S(1)}, u32[]{:S(2)}, u32[]{:S(2)}) collective-permute-start(f32[3,8,153]{2,1,0:T(8,128)S(1)} %pad_maximum_fusion.2), channel_id=1, source_target_pairs={{0,12},{4,0},{8,4},{12,8},{1,13},{5,1},{9,5},{13,9},{2,14},{6,2},{... | collective-permute-start | bytes 44072 | tf_op jit(solution)/shard_map/ppermute | solution.py:22
  49.8 1.2 collective-permute-start.8
  56.2 1.2 collective-permute-start.9
  57.6 5.8 %collective-permute-start.10 = (f32[3,8,153]{2,1,0:T(8,128)S(1)}, f32[3,8,153]{2,1,0:T(8,128)S(1)}, u32[]{:S(2)}, u32[]{:S(2)}) collective-permute-start(f32[3,8,153]{2,1,0:T(8,128)S(1)} %pad_maximum_fusion.3), channel_id=1, source_target_pairs={{0,4},{4,8},{8,12},{12,0},{1,5},{5,9},{9,13},{13,1},{2,6},{6,10},{... | collective-permute-start | bytes 44072 | tf_op jit(solution)/shard_map/ppermute | solution.py:22
  63.5 3.7 %collective-permute-start.11 = (f32[3,8,34]{2,1,0:T(8,128)S(1)}, f32[3,8,34]{2,1,0:T(8,128)S(1)}, u32[]{:S(2)}, u32[]{:S(2)}) collective-permute-start(f32[3,8,34]{2,1,0:T(8,128)S(1)} %pad_maximum_fusion.15), channel_id=1, source_target_pairs={{0,2},{2,0},{1,3},{3,1},{4,6},{6,4},{5,7},{7,5},{8,10},{10,8},{9,1... | collective-permute-start | bytes 9800 | tf_op jit(solution)/shard_map/ppermute | solution.py:22
  76.7 3.7 %collective-permute-start.12 = (f32[3,8,34]{2,1,0:T(8,128)S(1)}, f32[3,8,34]{2,1,0:T(8,128)S(1)}, u32[]{:S(2)}, u32[]{:S(2)}) collective-permute-start(f32[3,8,34]{2,1,0:T(8,128)S(1)} %pad_maximum_fusion.16), channel_id=1, source_target_pairs={{0,2},{2,0},{1,3},{3,1},{4,6},{6,4},{5,7},{7,5},{8,10},{10,8},{9,1... | collective-permute-start | bytes 9800 | tf_op jit(solution)/shard_map/ppermute | solution.py:22
  80.6 3.8 %collective-permute-start.13 = (f32[3,8,153]{2,1,0:T(8,128)S(1)}, f32[3,8,153]{2,1,0:T(8,128)S(1)}, u32[]{:S(2)}, u32[]{:S(2)}) collective-permute-start(f32[3,8,153]{2,1,0:T(8,128)S(1)} %pad_maximum_fusion.4), channel_id=1, source_target_pairs={{0,12},{4,0},{8,4},{12,8},{1,13},{5,1},{9,5},{13,9},{2,14},{6,2},{... | collective-permute-start | bytes 44072 | tf_op jit(solution)/shard_map/ppermute | solution.py:22
  84.6 1.2 collective-permute-start.14
  91.0 1.2 collective-permute-start.15
  92.4 5.6 %collective-permute-start.16 = (f32[3,8,153]{2,1,0:T(8,128)S(1)}, f32[3,8,153]{2,1,0:T(8,128)S(1)}, u32[]{:S(2)}, u32[]{:S(2)}) collective-permute-start(f32[3,8,153]{2,1,0:T(8,128)S(1)} %pad_maximum_fusion.5), channel_id=1, source_target_pairs={{0,4},{4,8},{8,12},{12,0},{1,5},{5,9},{9,13},{13,1},{2,6},{6,10},{... | collective-permute-start | bytes 44072 | tf_op jit(solution)/shard_map/ppermute | solution.py:22
  98.2 3.7 %collective-permute-start.17 = (f32[3,8,34]{2,1,0:T(8,128)S(1)}, f32[3,8,34]{2,1,0:T(8,128)S(1)}, u32[]{:S(2)}, u32[]{:S(2)}) collective-permute-start(f32[3,8,34]{2,1,0:T(8,128)S(1)} %pad_maximum_fusion.19), channel_id=1, source_target_pairs={{0,2},{2,0},{1,3},{3,1},{4,6},{6,4},{5,7},{7,5},{8,10},{10,8},{9,1... | collective-permute-start | bytes 9800 | tf_op jit(solution)/shard_map/ppermute | solution.py:22
  110.5 35.4 %copy-start.2 = (f32[3,8,128]{2,1,0:T(8,128)}, f32[3,8,128]{2,1,0:T(8,128)S(1)}, u32[]{:S(2)}) copy-start(f32[3,8,128]{2,1,0:T(8,128)S(1)} %pad_add_fusion) | copy-start | bytes 36868
  111.9 3.7 %collective-permute-start.18 = (f32[3,8,34]{2,1,0:T(8,128)S(1)}, f32[3,8,34]{2,1,0:T(8,128)S(1)}, u32[]{:S(2)}, u32[]{:S(2)}) collective-permute-start(f32[3,8,34]{2,1,0:T(8,128)S(1)} %pad_maximum_fusion.20), channel_id=1, source_target_pairs={{0,2},{2,0},{1,3},{3,1},{4,6},{6,4},{5,7},{7,5},{8,10},{10,8},{9,1... | collective-permute-start | bytes 9800 | tf_op jit(solution)/shard_map/ppermute | solution.py:22
  115.9 4.0 %collective-permute-start.19 = (f32[3,8,153]{2,1,0:T(8,128)S(1)}, f32[3,8,153]{2,1,0:T(8,128)S(1)}, u32[]{:S(2)}, u32[]{:S(2)}) collective-permute-start(f32[3,8,153]{2,1,0:T(8,128)S(1)} %pad_maximum_fusion.6), channel_id=1, source_target_pairs={{0,12},{4,0},{8,4},{12,8},{1,13},{5,1},{9,5},{13,9},{2,14},{6,2},{... | collective-permute-start | bytes 44072 | tf_op jit(solution)/shard_map/ppermute | solution.py:22
  120.1 1.2 collective-permute-start.20
  127.3 1.2 collective-permute-start.21
  128.8 5.6 %collective-permute-start.22 = (f32[3,8,153]{2,1,0:T(8,128)S(1)}, f32[3,8,153]{2,1,0:T(8,128)S(1)}, u32[]{:S(2)}, u32[]{:S(2)}) collective-permute-start(f32[3,8,153]{2,1,0:T(8,128)S(1)} %pad_maximum_fusion.7), channel_id=1, source_target_pairs={{0,4},{4,8},{8,12},{12,0},{1,5},{5,9},{9,13},{13,1},{2,6},{6,10},{... | collective-permute-start | bytes 44072 | tf_op jit(solution)/shard_map/ppermute | solution.py:22
  134.5 3.7 %collective-permute-start.23 = (f32[3,8,34]{2,1,0:T(8,128)S(1)}, f32[3,8,34]{2,1,0:T(8,128)S(1)}, u32[]{:S(2)}, u32[]{:S(2)}) collective-permute-start(f32[3,8,34]{2,1,0:T(8,128)S(1)} %pad_maximum_fusion.23), channel_id=1, source_target_pairs={{0,2},{2,0},{1,3},{3,1},{4,6},{6,4},{5,7},{7,5},{8,10},{10,8},{9,1... | collective-permute-start | bytes 9800 | tf_op jit(solution)/shard_map/ppermute | solution.py:22
where the time goes:
time: 179 us
  waiting for transfers between devices  50.2 us (28%)
  other arithmetic  38.8 us (22%)
  blocking collectives  29.9 us (17%)
  starting transfers between devices  25.1 us (14%)
  matrix products  15.5 us (9%)
  local copies, waits for them, and re-layouts  13.6 us (8%)
  between operations  5.39 us (3%)
    ppermute x24, waiting for transfers between devices, from_behind(): lax.ppermute(value, axis, [(i, (i + by) % count) for i in range(count)])  50.2 us
    psum x1, blocking collectives, on_device(): energies = lax.psum(energies, ('gx', 'gy', 'gz'))  29.9 us
    scatter-add x4, other arithmetic, local_forces(): home_forces = forces[:, :, :cluster_count].at[:, :, send_list].add(returned)  28.6 us
    ppermute x24, starting transfers between devices, from_behind(): lax.ppermute(value, axis, [(i, (i + by) % count) for i in range(count)])  25.1 us
    slice x92, local copies, waits for them, and re-layouts, split_blocks(): pieces.append(packed[:, :, position:position + length])  4.99 us
    dot_general x4, matrix products, domain_forces(): lax.dot_general(on_first, tables[0], contract, precision=lax.Precision.HI...  4.36 us
    dot_general x4, matrix products, domain_forces(): lax.dot_general(on_second, tables[1], contract, precision=lax.Precision.H...  4.27 us
    gather x8, local copies, waits for them, and re-layouts, share_coords(): outgoing = split_blocks(jnp.take(coords, send_list, axis=2), sizes_all)  3.98 us
  transfers between devices with their start and end apart: 24, of which 24 were waited for; matrix products, arithmetic and copies ran while one was open for 1% of the time, Pallas kernels for 0%

commit v1 on v0

v1 whole, which is shorter than its diff:
```python
import functools
import itertools

import jax
import jax.numpy as jnp
from jax import lax
from jax.experimental import pallas as pl
from jax.experimental.pallas import tpu as pltpu
from jax.sharding import PartitionSpec as P

CX = 1
CY = 8
CZ = 16
ITERS = 3
NORDER = 4
NITER = 1

MESH = pl.DeviceIdType.MESH
AXES = ("gx", "gy", "gz")
LANES = 128

time_step = 0.02
strength = 2.0
root_half = 0.7071067811865476
zone_list = ((1, 0, 0), (0, 1, 0), (0, 0, 1), (1, 1, 0), (1, 0, 1), (0, 1, 1), (1, 1, 1))


def zone_sizes():
    return tuple(
        (CX if d[0] == 0 else 1) * (CY if d[1] == 0 else 1) * (CZ if d[2] == 0 else 1)
        for d in zone_list
    )


def zone_spans():
    spans = []
    position = 0
    for size in zone_sizes()[1:]:
        spans.append((position, position + size))
        position += size
    return spans


def neighbour(sizes, direction, sign):
    ids = {}
    for axis, size, step in zip(AXES, sizes, direction):
        if step:
            ids[axis] = lax.rem(lax.axis_index(axis) + (size + sign * step), size)
    return ids


def peer(sizes, number):
    _, ny, nz = sizes
    steps = (number // (ny * nz), (number // nz) % ny, number % nz)
    return {
        axis: lax.rem(lax.axis_index(axis) + step, size)
        for axis, size, step in zip(AXES, sizes, steps)
    }


def each_peer(sizes, body):
    count = sizes[0] * sizes[1] * sizes[2]
    if count <= 32:
        for number in range(1, count):
            body(number)
    else:

        def step(number, carry):
            body(number)
            return carry

        lax.fori_loop(1, count, step, 0)


def up(value):
    return pltpu.roll(value, 7, 0)


def down(value):
    return pltpu.roll(value, 1, 0)


def dot3(a, b):
    return a[0] * b[0] + a[1] * b[1] + a[2] * b[2]


def expand(coupling, source):
    coupling_down = down(coupling)
    series = source
    result = source
    for _ in range(NORDER):
        series = coupling_down * down(series) + coupling * up(series)
        result = result + series
    return result


def apply_links(coords, directions, solution):
    scaled = root_half * solution
    moved = []
    for c in range(3):
        shift = directions[c] * scaled
        moved.append(coords[c] - shift + down(shift))
    return moved


def take_lanes(value, lanes):
    return jnp.take_along_axis(value, lanes, axis=1, mode="promise_in_bounds")


def merge_zones(parts, fill):
    lane = lax.broadcasted_iota(jnp.int32, (8, LANES), 1)
    spans = zone_spans()
    merged = fill
    for number in reversed(range(6)):
        low, high = spans[number]
        merged = jnp.where((lane >= low) & (lane < high), parts[number], merged)
    return merged


def halo_offset(c):
    lane = lax.broadcasted_iota(jnp.int32, (8, LANES), 1)
    offset = jnp.zeros((8, LANES), jnp.float32)
    for number, (low, high) in enumerate(zone_spans()):
        if zone_list[number + 1][c]:
            offset = jnp.where(
                (lane >= low) & (lane < high), float((CX, CY, CZ)[c]), offset
            )
    return offset


def kernel(
    sizes,
    unroll,
    pos_ref,
    vel_ref,
    send_ref,
    pair_ref,
    flag_ref,
    out_x,
    out_v,
    out_e,
    table,
    home,
    weights,
    ext,
    zin,
    cout,
    fout,
    fin,
    fbuf,
    force,
    unit,
    couple,
    eacc,
    eout,
    ein,
    send_sem,
    recv_sem,
    fsend_sem,
    frecv_sem,
    esend_sem,
    erecv_sem,
):
    slots = pair_ref.shape[1]
    tiles = slots // LANES
    bead = lax.broadcasted_iota(jnp.int32, (8, LANES), 0)
    count = sizes[0] * sizes[1] * sizes[2]
    pad_index = 2 * LANES + zone_spans()[-1][1]

    barrier = pltpu.get_barrier_semaphore()

    def greet(number):
        pl.semaphore_signal(barrier, inc=1, device_id=peer(sizes, number), device_id_type=MESH)

    each_peer(sizes, greet)

    out_x[...] = pos_ref[...]
    out_v[...] = vel_ref[...]
    flags = jnp.concatenate(
        [flag_ref[...].astype(jnp.float32), jnp.zeros((1, LANES), jnp.float32)], axis=0
    )
    flags_up = up(flags)
    first = [pos_ref[c] for c in range(3)]
    links = [a - up(a) for a in first]
    rest = jnp.sqrt(dot3(links, links))

    pl.semaphore_wait(barrier, count - 1)

    def coord_copy(zone):
        return pltpu.make_async_remote_copy(
            src_ref=cout.at[0 if zone == 0 else 1],
            dst_ref=zin.at[zone],
            send_sem=send_sem.at[zone],
            recv_sem=recv_sem.at[zone],
            device_id=neighbour(sizes, zone_list[zone], -1),
            device_id_type=MESH,
        )

    def force_copy(zone):
        return pltpu.make_async_remote_copy(
            src_ref=fout.at[0 if zone == 0 else 1],
            dst_ref=fin.at[zone],
            send_sem=fsend_sem.at[zone],
            recv_sem=frecv_sem.at[zone],
            device_id=neighbour(sizes, zone_list[zone], 1),
            device_id_type=MESH,
        )

    order = (6, 3, 4, 0, 1, 5, 2)

    def evaluate():
        for half in (1, 0):
            lanes = jnp.broadcast_to(send_ref[half : half + 1, :], (8, LANES))
            for c in range(3):
                cout[half, c] = take_lanes(out_x[c], lanes)
        copies = [coord_copy(zone) for zone in range(7)]
        for zone in order:
            copies[zone].start()

    def prepare():
        old = [out_x[c] for c in range(3)]
        vectors = [a - up(a) for a in old]
        length = jnp.maximum(jnp.sqrt(dot3(vectors, vectors)), 0.2)
        directions = [a / length for a in vectors]
        for c in range(3):
            unit[c] = directions[c]
        couple[...] = 0.5 * dot3(directions, [up(a) for a in directions]) * flags * flags_up

    def build_tables():
        lane = lax.broadcasted_iota(jnp.int32, (LANES, LANES), 1)
        for half in range(2):
            rows = jnp.broadcast_to(send_ref[half : half + 1, :], (LANES, LANES)).T
            home[half * LANES : (half + 1) * LANES, :] = (
                (rows == lane).astype(jnp.float32).astype(jnp.bfloat16)
            )

        def build(tile, carry):
            at = pl.ds(pl.multiple_of(tile * LANES, LANES), LANES)
            for side in range(2):
                rows = jnp.broadcast_to(pair_ref[side : side + 1, at], (LANES, LANES)).T
                start = pl.multiple_of(side * slots + tile * LANES, LANES)
                for block in range(3):
                    table[pl.ds(start, LANES), block * LANES : (block + 1) * LANES] = (
                        (rows == lane + block * LANES).astype(jnp.float32).astype(jnp.bfloat16)
                    )
            one = jnp.broadcast_to(pair_ref[0:1, at], (8, LANES))
            two = jnp.broadcast_to(pair_ref[1:2, at], (8, LANES))
            for shift in range(8):
                use = one != two
                if shift:
                    use = use | (bead < 8 - shift)
                use = use & (one != pad_index)
                weights[tile, shift] = use.astype(jnp.float32)
            return carry

        lax.fori_loop(0, tiles, build, 0)

    def receive_coords():
        for c in range(3):
            ext[0, c] = out_x[c]
        copies = [coord_copy(zone) for zone in range(7)]
        for zone in range(7):
            copies[zone].wait()
        for c in range(3):
            ext[1, c] = zin[0, c] + float(CX if c == 0 else 0)
            merged = merge_zones(
                [zin[zone, c] for zone in range(1, 7)], jnp.zeros((8, LANES), jnp.float32)
            )
            ext[2, c] = merged + halo_offset(c)

    def pairs():
        def tile_step(tile, energy):
            at = pl.ds(pl.multiple_of(tile * LANES, LANES), LANES)
            beads = []
            for side in range(2):
                index = jnp.broadcast_to(pair_ref[side : side + 1, at], (8, LANES))
                lanes = index & (LANES - 1)
                in_own = index < LANES
                in_first = index < 2 * LANES
                beads.append(
                    [
                        jnp.where(
                            in_own,
                            take_lanes(ext[0, c], lanes),
                            jnp.where(
                                in_first,
                                take_lanes(ext[1, c], lanes),
                                take_lanes(ext[2, c], lanes),
                            ),
                        )
                        for c in range(3)
                    ]
                )
            on_first = [None] * 3
            on_second = [None] * 3
            for shift in range(8):
                gap = []
                for c in range(3):
                    other = beads[1][c]
                    if shift:
                        other = pltpu.roll(other, 8 - shift, 0)
                    gap.append(beads[0][c] - other)
                reach = jnp.maximum(weights[tile, shift] - dot3(gap, gap), 0.0)
                square = reach * reach
                energy = energy + square * reach
                for c in range(3):
                    push = square * gap[c]
                    back = pltpu.roll(push, shift, 0) if shift else push
                    on_first[c] = push if shift == 0 else on_first[c] + push
                    on_second[c] = -back if shift == 0 else on_second[c] - back
            for side, parts in enumerate((on_first, on_second)):
                start = pl.multiple_of(side * slots + tile * LANES, LANES)
                for c in range(3):
                    high = parts[c].astype(jnp.bfloat16).astype(jnp.float32)
                    fbuf[c * 8 : c * 8 + 8, pl.ds(start, LANES)] = high
                    fbuf[24 + c * 8 : 32 + c * 8, pl.ds(start, LANES)] = parts[c] - high
            return energy

        def group(number, energy):
            for inner in range(unroll):
                energy = tile_step(number * unroll + inner, energy)
            return energy

        return lax.fori_loop(0, tiles // unroll, group, jnp.zeros((8, LANES), jnp.float32))

    def scatter():
        values = fbuf[...].astype(jnp.bfloat16)
        halo = jnp.dot(values, table[:, LANES:], preferred_element_type=jnp.float32)
        halo = (6.0 * strength) * (halo[:24] + halo[24:])
        for half in (1, 0):
            for c in range(3):
                fout[half, c] = halo[c * 8 : c * 8 + 8, half * LANES : (half + 1) * LANES]
        copies = [force_copy(zone) for zone in range(7)]
        for zone in order:
            copies[zone].start()
        own = jnp.dot(values, table[:, :LANES], preferred_element_type=jnp.float32)
        own = (6.0 * strength) * (own[:24] + own[24:])
        for zone in range(7):
            copies[zone].wait()
        zero = jnp.zeros((8, LANES), jnp.float32)
        rows = []
        for c in range(3):
            merged = merge_zones([fin[zone, c] for zone in range(1, 7)], zero)
            rows.append(jnp.concatenate([fin[0, c], merged], axis=1))
        back = jnp.concatenate(rows, axis=0)
        high = back.astype(jnp.bfloat16).astype(jnp.float32)
        split = jnp.concatenate([high, back - high], axis=0).astype(jnp.bfloat16)
        added = jnp.dot(split, home[...], preferred_element_type=jnp.float32)
        total = own + added[:24] + added[24:]
        for c in range(3):
            force[c] = total[c * 8 : c * 8 + 8]

    def integrate():
        old = [out_x[c] for c in range(3)]
        half = [out_v[c] + (0.5 * time_step) * force[c] for c in range(3)]
        moved = [old[c] + time_step * half[c] for c in range(3)]
        directions = [unit[c] for c in range(3)]
        coupling = couple[...]
        vectors = [a - up(a) for a in moved]
        projected = dot3(directions, vectors)
        solved = expand(coupling, flags * root_half * (projected - rest))
        moved = apply_links(moved, directions, solved)
        for _ in range(NITER):
            vectors = [a - up(a) for a in moved]
            squared = dot3(vectors, vectors)
            target = jnp.sqrt(jnp.maximum(2.0 * rest * rest - squared, 0.25 * rest * rest))
            solved = expand(coupling, flags * root_half * (rest - target))
            moved = apply_links(moved, directions, solved)
        for c in range(3):
            out_v[c] = (moved[c] - old[c]) / time_step
            out_x[c] = moved[c]

    def step(number, carry):
        @pl.when(number > 0)
        def _():
            integrate()

        evaluate()
        prepare()

        @pl.when(number == 0)
        def _():
            build_tables()

        receive_coords()
        energy = pairs()
        scatter()

        @pl.when(number > 0)
        def _():
            speeds = [out_v[c] + (0.5 * time_step) * force[c] for c in range(3)]
            for c in range(3):
                out_v[c] = speeds[c]
            eacc[2 * (number - 1)] = strength * energy
            eacc[2 * (number - 1) + 1] = 0.5 * dot3(speeds, speeds)

        return carry

    lax.fori_loop(0, ITERS + 1, step, 0)

    total = jnp.zeros((8, LANES), jnp.float32)
    for row in range(2 * ITERS):
        line = jnp.sum(eacc[row], axis=0, keepdims=True)
        total = jnp.where(bead == row, line, total)
    eout[...] = total

    def energy_copy(number):
        return pltpu.make_async_remote_copy(
            src_ref=eout,
            dst_ref=ein.at[number],
            send_sem=esend_sem.at[number],
            recv_sem=erecv_sem.at[number],
            device_id=peer(sizes, number),
            device_id_type=MESH,
        )

    each_peer(sizes, lambda number: energy_copy(number).start())
    each_peer(sizes, lambda number: energy_copy(number).wait())
    if count <= 32:
        for number in range(1, count):
            total = total + ein[number]
    else:
        total = lax.fori_loop(1, count, lambda number, acc: acc + ein[number], total)
    beads = 8 * LANES * count
    summed = jnp.sum(total, axis=1, keepdims=True) / beads
    for row in range(ITERS):
        for column in range(2):
            at = 2 * row + column
            out_e[row : row + 1, column : column + 1] = summed[at : at + 1, :]


def on_device(sizes, positions, velocities, send_list, pair_list, constraint_flags):
    clusters = positions.shape[2]
    slots = pair_list.shape[1]
    tiles = slots // LANES
    count = sizes[0] * sizes[1] * sizes[2]
    unroll = max(u for u in range(1, 8) if tiles % u == 0)
    sends = jnp.pad(send_list, (0, 2 * LANES - send_list.shape[0])).reshape(2, LANES)
    vmem = pl.BlockSpec(memory_space=pltpu.VMEM)
    f32 = jnp.float32
    return pl.pallas_call(
        functools.partial(kernel, sizes, unroll),
        out_shape=(
            jax.ShapeDtypeStruct(positions.shape, f32),
            jax.ShapeDtypeStruct(velocities.shape, f32),
            jax.ShapeDtypeStruct((ITERS, 2), f32),
        ),
        in_specs=[vmem] * 5,
        out_specs=(vmem, vmem, vmem),
        scratch_shapes=[
            pltpu.VMEM((2 * slots, 3 * clusters), jnp.bfloat16),
            pltpu.VMEM((2 * clusters, clusters), jnp.bfloat16),
            pltpu.VMEM((tiles, 8, 8, LANES), f32),
            pltpu.VMEM((3, 3, 8, LANES), f32),
            pltpu.VMEM((7, 3, 8, LANES), f32),
            pltpu.VMEM((2, 3, 8, LANES), f32),
            pltpu.VMEM((2, 3, 8, LANES), f32),
            pltpu.VMEM((7, 3, 8, LANES), f32),
            pltpu.VMEM((48, 2 * slots), f32),
            pltpu.VMEM((3, 8, LANES), f32),
            pltpu.VMEM((3, 8, LANES), f32),
            pltpu.VMEM((8, LANES), f32),
            pltpu.VMEM((2 * ITERS, 8, LANES), f32),
            pltpu.VMEM((8, LANES), f32),
            pltpu.VMEM((count, 8, LANES), f32),
            pltpu.SemaphoreType.DMA((7,)),
            pltpu.SemaphoreType.DMA((7,)),
            pltpu.SemaphoreType.DMA((7,)),
            pltpu.SemaphoreType.DMA((7,)),
            pltpu.SemaphoreType.DMA((count,)),
            pltpu.SemaphoreType.DMA((count,)),
        ],
        compiler_params=pltpu.CompilerParams(collective_id=0, has_side_effects=True),
    )(positions, velocities, sends, pair_list, constraint_flags)


def solution(mesh):
    sizes = tuple(mesh.shape[axis] for axis in AXES)
    split = ("runs", "gx", "gy", "gz")
    return jax.shard_map(
        functools.partial(on_device, sizes),
        mesh=mesh,
        in_specs=(
            P(None, None, split),
            P(None, None, split),
            P(split),
            P(None, split),
            P(None, split),
        ),
        out_specs=(P(None, None, split), P(None, None, split), P("runs", None)),
        check_vma=False,
    )
```

time: 179 us -> 55.4 us (0.31)
  waiting for transfers between devices: 50.2 us -> 0 us
  Pallas kernels: 0 us -> 50 us
  other arithmetic: 38.8 us -> 0 us
  blocking collectives: 29.9 us -> 0 us
  starting transfers between devices: 25.1 us -> 0 us
  matrix products: 15.5 us -> 0 us
  local copies, waits for them, and re-layouts: 13.6 us -> 4.47 us
  between operations: 5.39 us -> 0.65 us
    ppermute x24 -> x0, waiting for transfers between devices: 50.2 us -> none  [from_behind(): lax.ppermute(value, axis, [(i, (i + by) % count) for i in range(count)])]
    pallas_call x0 -> x1, Pallas kernels: none -> 50 us  [on_device(): pl.pallas_call(functools.partial(kernel, sizes, unroll), out_shape=(jax.S...]
    psum x1 -> x0, blocking collectives: 29.9 us -> none  [on_device(): energies = lax.psum(energies, ('gx', 'gy', 'gz'))]
    scatter-add x4 -> x0, other arithmetic: 28.6 us -> none  [local_forces(): home_forces = forces[:, :, :cluster_count].at[:, :, send_list].add(returned)]
    ppermute x24 -> x0, starting transfers between devices: 25.1 us -> none  [from_behind(): lax.ppermute(value, axis, [(i, (i + by) % count) for i in range(count)])]
    dot_general x16 -> x0, matrix products: 15.5 us -> none  [the longest x4 4.36 us: domain_forces(): lax.dot_general(on_first, tables[0], contract, precision=lax.Precision.HI...]
    reduce_sum x23 -> x0, other arithmetic: 5.62 us -> none  [the longest x4 1.95 us: domain_forces(): on_first = jnp.sum(pushing, axis=2).reshape(24, slot_count)]
    slice x93 -> x0, local copies, waits for them, and re-layouts: 5.03 us -> none  [the longest x92 4.99 us: split_blocks(): pieces.append(packed[:, :, position:position + length])]
  transfers between devices with their start and end apart: 24 -> 0, of which waited for: 24 -> 0; matrix products, arithmetic and copies ran while one was open for 1% -> 0% of each run, Pallas kernels for 0% -> 0%
where the time goes in v1:
time: 55.4 us; the launch traced here: 55.1 us
  Pallas kernels  50 us (90%)
  local copies, waits for them, and re-layouts  4.47 us (8%)
  between operations  0.65 us (1%)
    pallas_call x1, Pallas kernels, on_device(): pl.pallas_call(functools.partial(kernel, sizes, unroll), out_shape=(jax.S...  50 us
    unnamed x6, local copies, waits for them, and re-layouts  2.58 us
    reshape x1, local copies, waits for them, and re-layouts, on_device(): jnp.pad(send_list, (0, 2 * LANES - send_list.shape[0])).reshape(2, LANES)  1.24 us

profile of v1, /device:TPU:0, one launch (start us, length us, event | category | flops | bytes accessed | tf_op | source)
XLA Modules:
  0.0 55.1 jit_solution(8976850497223972018)
XLA Ops:
  0.6 1.2 %pad_bitcast_fusion.send_ref = s32[2,128]{1,0:T(2,128)} fusion(s32[178]{0:T(256)} %param.7), kind=kLoop, calls=%fused_computation | loop fusion | bytes 1736 | tf_op jit(solution)/shard_map/reshape | solution.py:438
  1.9 50.0 %shard_map.76 = (f32[3,8,128]{2,1,0:T(8,128)}, f32[3,8,128]{2,1,0:T(8,128)}, f32[3,2]{1,0:T(4,128)}) custom-call(f32[3,8,128]{2,1,0:T(8,128)} %pos_ref.1, f32[3,8,128]{2,1,0:T(8,128)} %vel_ref.1, s32[2,128]{1,0:T(2,128)} %pad_bitcast_fusion.send_ref, s32[2,1792]{1,0:T(2,128)} %pair_ref.1, s32[7,128]{1,0:T(8,128)} %flag_ref.1), custom_call_target="tpu_custom_call" | custom-call | tf_op jit(solution)/shard_map/pallas_call | solution.py:441
  51.9 0.0 copy-start.1
  51.9 0.7 %copy-done.1 = f32[3,2]{1,0:T(4,128)S(1)} copy-done((f32[3,2]{1,0:T(4,128)S(1)}, f32[3,2]{1,0:T(4,128)}, u32[]{:S(2)}) %copy-start.1) | copy-done | bytes 48
  52.6 0.6 %copy.8 = f32[3,2]{0,1:T(2,128)} copy(f32[3,2]{1,0:T(4,128)S(1)} %copy-done.1) | data formatting | bytes 48 | tf_op jit(solution)/shard_map/pallas_call | solution.py:441
  53.2 0.0 copy-start
  53.2 1.3 %copy.11 = f32[3,8,128]{2,1,0:T(8,128)} copy(f32[3,8,128]{2,1,0:T(8,128)} %get-tuple-element.9) | data formatting | bytes 24576
  54.5 0.0 copy-done
  54.5 0.6 %copy.12 = f32[3,8,128]{2,1,0:T(8,128)} copy(f32[3,8,128]{2,1,0:T(8,128)S(1)} %copy-done) | data formatting | bytes 24576
Async XLA Ops:
  51.9 0.7 %copy-start.1 = (f32[3,2]{1,0:T(4,128)S(1)}, f32[3,2]{1,0:T(4,128)}, u32[]{:S(2)}) copy-start(f32[3,2]{1,0:T(4,128)} %get-tuple-element.5) | copy-start | bytes 76
  53.2 1.3 %copy-start = (f32[3,8,128]{2,1,0:T(8,128)S(1)}, f32[3,8,128]{2,1,0:T(8,128)}, u32[]{:S(2)}) copy-start(f32[3,8,128]{2,1,0:T(8,128)} %get-tuple-element.10) | copy-start | bytes 36868

commit v2 on v1

--- a/solution.py
+++ b/solution.py
@@ -131,14 +131,19 @@
 def kernel(
     sizes,
     unroll,
-    pos_ref,
-    vel_ref,
+    pos_hbm,
+    vel_hbm,
+    send_hbm,
+    pair_hbm,
+    flag_hbm,
+    out_x,
+    out_v,
+    out_e,
+    send_flat,
     send_ref,
     pair_ref,
     flag_ref,
-    out_x,
-    out_v,
-    out_e,
+    load_sem,
     table,
     home,
     weights,
@@ -174,13 +179,32 @@
 
     each_peer(sizes, greet)
 
-    out_x[...] = pos_ref[...]
-    out_v[...] = vel_ref[...]
+    loads = [
+        pltpu.make_async_copy(source, target, load_sem.at[number])
+        for number, (source, target) in enumerate(
+            (
+                (pos_hbm, out_x),
+                (send_hbm, send_flat),
+                (pair_hbm, pair_ref),
+                (flag_hbm, flag_ref),
+                (vel_hbm, out_v),
+            )
+        )
+    ]
+    for load in loads:
+        load.start()
+    for load in loads:
+        load.wait()
+    small = send_flat.shape[0] - LANES
+    send_ref[0:1, :] = send_flat[0:LANES].reshape(1, LANES)
+    send_ref[1:2, :] = jnp.concatenate(
+        [send_flat[LANES:], jnp.zeros((LANES - small,), jnp.int32)]
+    ).reshape(1, LANES)
     flags = jnp.concatenate(
         [flag_ref[...].astype(jnp.float32), jnp.zeros((1, LANES), jnp.float32)], axis=0
     )
     flags_up = up(flags)
-    first = [pos_ref[c] for c in range(3)]
+    first = [out_x[c] for c in range(3)]
     links = [a - up(a) for a in first]
     rest = jnp.sqrt(dot3(links, links))
 
@@ -426,7 +450,13 @@
     for row in range(ITERS):
         for column in range(2):
             at = 2 * row + column
-            out_e[row : row + 1, column : column + 1] = summed[at : at + 1, :]
+            out_e[column : column + 1, row : row + 1] = summed[at : at + 1, :]
+
+
+def finish(coords, speeds, sums, out_x, out_v, out_e):
+    out_x[...] = coords[...]
+    out_v[...] = speeds[...]
+    out_e[...] = sums[...]
 
 
 def on_device(sizes, positions, velocities, send_list, pair_list, constraint_flags):
@@ -435,19 +465,23 @@
     tiles = slots // LANES
     count = sizes[0] * sizes[1] * sizes[2]
     unroll = max(u for u in range(1, 8) if tiles % u == 0)
-    sends = jnp.pad(send_list, (0, 2 * LANES - send_list.shape[0])).reshape(2, LANES)
     vmem = pl.BlockSpec(memory_space=pltpu.VMEM)
     f32 = jnp.float32
-    return pl.pallas_call(
+    coords, speeds, sums = pl.pallas_call(
         functools.partial(kernel, sizes, unroll),
         out_shape=(
             jax.ShapeDtypeStruct(positions.shape, f32),
             jax.ShapeDtypeStruct(velocities.shape, f32),
-            jax.ShapeDtypeStruct((ITERS, 2), f32),
+            jax.ShapeDtypeStruct((2, ITERS), f32),
         ),
-        in_specs=[vmem] * 5,
+        in_specs=[pl.BlockSpec(memory_space=pl.ANY)] * 5,
         out_specs=(vmem, vmem, vmem),
         scratch_shapes=[
+            pltpu.VMEM(send_list.shape, jnp.int32),
+            pltpu.VMEM((2, LANES), jnp.int32),
+            pltpu.VMEM(pair_list.shape, jnp.int32),
+            pltpu.VMEM(constraint_flags.shape, jnp.int32),
+            pltpu.SemaphoreType.DMA((5,)),
             pltpu.VMEM((2 * slots, 3 * clusters), jnp.bfloat16),
             pltpu.VMEM((2 * clusters, clusters), jnp.bfloat16),
             pltpu.VMEM((tiles, 8, 8, LANES), f32),
@@ -471,7 +505,15 @@
             pltpu.SemaphoreType.DMA((count,)),
         ],
         compiler_params=pltpu.CompilerParams(collective_id=0, has_side_effects=True),
-    )(positions, velocities, sends, pair_list, constraint_flags)
+    )(positions, velocities, send_list, pair_list, constraint_flags)
+    results = (coords, speeds, sums)
+    coords, speeds, sums = pl.pallas_call(
+        finish,
+        out_shape=tuple(jax.ShapeDtypeStruct(r.shape, f32) for r in results),
+        in_specs=[vmem] * 3,
+        out_specs=(vmem, vmem, vmem),
+    )(*results)
+    return coords, speeds, sums.T
 
 
 def solution(mesh):

time: 55.4 us -> 51.7 us (0.933)
  local copies, waits for them, and re-layouts: 4.47 us -> 0 us
  Pallas kernels: 50 us -> 50.7 us
    unnamed x6 -> x0, local copies, waits for them, and re-layouts: 2.58 us -> none
    pallas_call x0 -> x1, Pallas kernels: none -> 1.33 us  [on_device(): pl.pallas_call(finish, out_shape=tuple((jax.ShapeDtypeStruct(r.shape, f32...]
    reshape x1 -> x0, local copies, waits for them, and re-layouts: 1.24 us -> none  [on_device(): jnp.pad(send_list, (0, 2 * LANES - send_list.shape[0])).reshape(2, LANES)]
    pallas_call x1 -> x0, local copies, waits for them, and re-layouts: 0.65 us -> none  [on_device(): pl.pallas_call(functools.partial(kernel, sizes, unroll), out_shape=(jax.S...]
    pallas_call x1, Pallas kernels: 50 us -> 49.4 us  [on_device(): pl.pallas_call(functools.partial(kernel, sizes, unroll), out_shape=(jax.S...]
where the time goes in v2:
time: 51.7 us; the launch traced here: 51.3 us
  Pallas kernels  50.7 us (98%)
  between operations  0.64 us (1%)
    pallas_call x1, Pallas kernels, on_device(): pl.pallas_call(functools.partial(kernel, sizes, unroll), out_shape=(jax.S...  49.4 us
    pallas_call x1, Pallas kernels, on_device(): pl.pallas_call(finish, out_shape=tuple((jax.ShapeDtypeStruct(r.shape, f32...  1.33 us

profile of v2, /device:TPU:0, one launch (start us, length us, event | category | flops | bytes accessed | tf_op | source)
XLA Modules:
  0.0 51.3 jit_solution(13654680776949381473)
XLA Ops:
  0.6 49.4 %shard_map.76 = (f32[3,8,128]{2,1,0:T(8,128)}, f32[3,8,128]{2,1,0:T(8,128)}, f32[2,3]{1,0:T(2,128)}) custom-call(f32[3,8,128]{2,1,0:T(8,128)} %pos_hbm.1, f32[3,8,128]{2,1,0:T(8,128)} %vel_hbm.1, s32[178]{0:T(256)} %send_hbm.1, s32[2,1792]{1,0:T(2,128)} %pair_hbm.1, s32[7,128]{1,0:T(8,128)} %flag_hbm.1), custom_call_target="tpu_custom_call" | custom-call | tf_op jit(solution)/shard_map/pallas_call | solution.py:470
  50.0 1.3 %shard_map.77 = (f32[3,8,128]{2,1,0:T(8,128)}, f32[3,8,128]{2,1,0:T(8,128)}, f32[2,3]{1,0:T(2,128)}) custom-call(f32[3,8,128]{2,1,0:T(8,128)} %get-tuple-element.9.coords, f32[3,8,128]{2,1,0:T(8,128)} %get-tuple-element.10.speeds, f32[2,3]{1,0:T(2,128)} %get-tuple-element.11.sums), custom_call_target="tpu_custom_call" | custom-call | tf_op jit(solution)/shard_map/pallas_call | solution.py:510

commit v3 on v2

--- a/solution.py
+++ b/solution.py
@@ -18,6 +18,7 @@
 MESH = pl.DeviceIdType.MESH
 AXES = ("gx", "gy", "gz")
 LANES = 128
+WIDTH = LANES // 8
 
 time_step = 0.02
 strength = 2.0
@@ -107,13 +108,21 @@
     return jnp.take_along_axis(value, lanes, axis=1, mode="promise_in_bounds")
 
 
-def merge_zones(parts, fill):
+def pack_zone(value, lanes):
+    bead = lax.broadcasted_iota(jnp.int32, (8, LANES), 0)
     lane = lax.broadcasted_iota(jnp.int32, (8, LANES), 1)
-    spans = zone_spans()
-    merged = fill
-    for number in reversed(range(6)):
-        low, high = spans[number]
-        merged = jnp.where((lane >= low) & (lane < high), parts[number], merged)
+    chosen = jnp.where(lane // WIDTH == bead, take_lanes(value, lanes), 0.0)
+    return jnp.sum(chosen, axis=0, keepdims=True)
+
+
+def merge_zones(rows):
+    bead = lax.broadcasted_iota(jnp.int32, (8, LANES), 0)
+    lane = lax.broadcasted_iota(jnp.int32, (8, LANES), 1)
+    merged = jnp.zeros((8, LANES), jnp.float32)
+    for row, (low, high) in zip(rows, zone_spans()):
+        lanes = bead * WIDTH + jnp.clip(lane - low, 0, WIDTH - 1)
+        spread = take_lanes(jnp.broadcast_to(row, (8, LANES)), lanes)
+        merged = jnp.where((lane >= low) & (lane < high), spread, merged)
     return merged
 
 
@@ -148,10 +157,15 @@
     home,
     weights,
     ext,
+    picks,
     zin,
+    zmsg,
     cout,
+    cmsg,
     fout,
+    fmsg,
     fin,
+    finmsg,
     fbuf,
     force,
     unit,
@@ -208,12 +222,17 @@
     links = [a - up(a) for a in first]
     rest = jnp.sqrt(dot3(links, links))
 
+    lane = lax.broadcasted_iota(jnp.int32, (8, LANES), 1)
+    listed = jnp.broadcast_to(send_ref[1:2, :], (8, LANES))
+    for number, (low, _) in enumerate(zone_spans()):
+        picks[number] = take_lanes(listed, low + lane % WIDTH)
+
     pl.semaphore_wait(barrier, count - 1)
 
     def coord_copy(zone):
         return pltpu.make_async_remote_copy(
-            src_ref=cout.at[0 if zone == 0 else 1],
-            dst_ref=zin.at[zone],
+            src_ref=cmsg.at[zone - 1] if zone else cout,
+            dst_ref=zmsg.at[zone - 1] if zone else zin,
             send_sem=send_sem.at[zone],
             recv_sem=recv_sem.at[zone],
             device_id=neighbour(sizes, zone_list[zone], -1),
@@ -222,24 +241,27 @@
 
     def force_copy(zone):
         return pltpu.make_async_remote_copy(
-            src_ref=fout.at[0 if zone == 0 else 1],
-            dst_ref=fin.at[zone],
+            src_ref=fmsg.at[zone - 1] if zone else fout,
+            dst_ref=finmsg.at[zone - 1] if zone else fin,
             send_sem=fsend_sem.at[zone],
             recv_sem=frecv_sem.at[zone],
             device_id=neighbour(sizes, zone_list[zone], 1),
             device_id_type=MESH,
         )
 
-    order = (6, 3, 4, 0, 1, 5, 2)
+    order = (3, 0, 6, 4, 1, 5, 2)
+    lane = lax.broadcasted_iota(jnp.int32, (8, LANES), 1)
+    inside = [low + lane % WIDTH for low, _ in zone_spans()]
 
     def evaluate():
-        for half in (1, 0):
-            lanes = jnp.broadcast_to(send_ref[half : half + 1, :], (8, LANES))
+        lanes = jnp.broadcast_to(send_ref[0:1, :], (8, LANES))
+        for zone in order:
             for c in range(3):
-                cout[half, c] = take_lanes(out_x[c], lanes)
-        copies = [coord_copy(zone) for zone in range(7)]
-        for zone in order:
-            copies[zone].start()
+                if zone:
+                    cmsg[zone - 1, c : c + 1, :] = pack_zone(out_x[c], picks[zone - 1])
+                else:
+                    cout[c] = take_lanes(out_x[c], lanes)
+            coord_copy(zone).start()
 
     def prepare():
         old = [out_x[c] for c in range(3)]
@@ -286,10 +308,8 @@
         for zone in range(7):
             copies[zone].wait()
         for c in range(3):
-            ext[1, c] = zin[0, c] + float(CX if c == 0 else 0)
-            merged = merge_zones(
-                [zin[zone, c] for zone in range(1, 7)], jnp.zeros((8, LANES), jnp.float32)
-            )
+            ext[1, c] = zin[c] + float(CX if c == 0 else 0)
+            merged = merge_zones([zmsg[number, c : c + 1, :] for number in range(6)])
             ext[2, c] = merged + halo_offset(c)
 
     def pairs():
@@ -351,21 +371,23 @@
         values = fbuf[...].astype(jnp.bfloat16)
         halo = jnp.dot(values, table[:, LANES:], preferred_element_type=jnp.float32)
         halo = (6.0 * strength) * (halo[:24] + halo[24:])
-        for half in (1, 0):
-            for c in range(3):
-                fout[half, c] = halo[c * 8 : c * 8 + 8, half * LANES : (half + 1) * LANES]
         copies = [force_copy(zone) for zone in range(7)]
         for zone in order:
+            for c in range(3):
+                rows = halo[c * 8 : c * 8 + 8]
+                if zone:
+                    fmsg[zone - 1, c : c + 1, :] = pack_zone(rows[:, LANES:], inside[zone - 1])
+                else:
+                    fout[c] = rows[:, :LANES]
             copies[zone].start()
         own = jnp.dot(values, table[:, :LANES], preferred_element_type=jnp.float32)
         own = (6.0 * strength) * (own[:24] + own[24:])
         for zone in range(7):
             copies[zone].wait()
-        zero = jnp.zeros((8, LANES), jnp.float32)
         rows = []
         for c in range(3):
-            merged = merge_zones([fin[zone, c] for zone in range(1, 7)], zero)
-            rows.append(jnp.concatenate([fin[0, c], merged], axis=1))
+            merged = merge_zones([finmsg[number, c : c + 1, :] for number in range(6)])
+            rows.append(jnp.concatenate([fin[c], merged], axis=1))
         back = jnp.concatenate(rows, axis=0)
         high = back.astype(jnp.bfloat16).astype(jnp.float32)
         split = jnp.concatenate([high, back - high], axis=0).astype(jnp.bfloat16)
@@ -486,10 +508,15 @@
             pltpu.VMEM((2 * clusters, clusters), jnp.bfloat16),
             pltpu.VMEM((tiles, 8, 8, LANES), f32),
             pltpu.VMEM((3, 3, 8, LANES), f32),
-            pltpu.VMEM((7, 3, 8, LANES), f32),
-            pltpu.VMEM((2, 3, 8, LANES), f32),
-            pltpu.VMEM((2, 3, 8, LANES), f32),
-            pltpu.VMEM((7, 3, 8, LANES), f32),
+            pltpu.VMEM((6, 8, LANES), jnp.int32),
+            pltpu.VMEM((3, 8, LANES), f32),
+            pltpu.VMEM((6, 3, LANES), f32),
+            pltpu.VMEM((3, 8, LANES), f32),
+            pltpu.VMEM((6, 3, LANES), f32),
+            pltpu.VMEM((3, 8, LANES), f32),
+            pltpu.VMEM((6, 3, LANES), f32),
+            pltpu.VMEM((3, 8, LANES), f32),
+            pltpu.VMEM((6, 3, LANES), f32),
             pltpu.VMEM((48, 2 * slots), f32),
             pltpu.VMEM((3, 8, LANES), f32),
             pltpu.VMEM((3, 8, LANES), f32),

time: 51.7 us -> 50.5 us (0.977)
  Pallas kernels: 50.7 us -> 49.5 us
    pallas_call x1, Pallas kernels: 49.4 us -> 48.2 us  [on_device(): pl.pallas_call(functools.partial(kernel, sizes, unroll), out_shape=(jax.S...]
where the time goes in v3:
time: 50.5 us; the launch traced here: 50.1 us
  Pallas kernels  49.5 us (98%)
  between operations  0.64 us (1%)
    pallas_call x1, Pallas kernels, on_device(): pl.pallas_call(functools.partial(kernel, sizes, unroll), out_shape=(jax.S...  48.2 us
    pallas_call x1, Pallas kernels, on_device(): pl.pallas_call(finish, out_shape=tuple((jax.ShapeDtypeStruct(r.shape, f32...  1.33 us

profile of v3, /device:TPU:0, one launch (start us, length us, event | category | flops | bytes accessed | tf_op | source)
XLA Modules:
  0.0 50.1 jit_solution(4363712022687715031)
XLA Ops:
  0.6 48.2 %shard_map.76 = (f32[3,8,128]{2,1,0:T(8,128)}, f32[3,8,128]{2,1,0:T(8,128)}, f32[2,3]{1,0:T(2,128)}) custom-call(f32[3,8,128]{2,1,0:T(8,128)} %pos_hbm.1, f32[3,8,128]{2,1,0:T(8,128)} %vel_hbm.1, s32[178]{0:T(256)} %send_hbm.1, s32[2,1792]{1,0:T(2,128)} %pair_hbm.1, s32[7,128]{1,0:T(8,128)} %flag_hbm.1), custom_call_target="tpu_custom_call" | custom-call | tf_op jit(solution)/shard_map/pallas_call | solution.py:492
  48.8 1.3 %shard_map.77 = (f32[3,8,128]{2,1,0:T(8,128)}, f32[3,8,128]{2,1,0:T(8,128)}, f32[2,3]{1,0:T(2,128)}) custom-call(f32[3,8,128]{2,1,0:T(8,128)} %get-tuple-element.9.coords, f32[3,8,128]{2,1,0:T(8,128)} %get-tuple-element.10.speeds, f32[2,3]{1,0:T(2,128)} %get-tuple-element.11.sums), custom_call_target="tpu_custom_call" | custom-call | tf_op jit(solution)/shard_map/pallas_call | solution.py:537

commit v4 on v3

--- a/solution.py
+++ b/solution.py
@@ -486,7 +486,7 @@
     slots = pair_list.shape[1]
     tiles = slots // LANES
     count = sizes[0] * sizes[1] * sizes[2]
-    unroll = max(u for u in range(1, 8) if tiles % u == 0)
+    unroll = max(u for u in range(1, 15) if tiles % u == 0)
     vmem = pl.BlockSpec(memory_space=pltpu.VMEM)
     f32 = jnp.float32
     coords, speeds, sums = pl.pallas_call(

time: 50.5 us -> 49.3 us (0.976)
  Pallas kernels: 49.5 us -> 48.3 us
    pallas_call x1, Pallas kernels: 48.2 us -> 47 us  [on_device(): pl.pallas_call(functools.partial(kernel, sizes, unroll), out_shape=(jax.S...]
where the time goes in v4:
time: 49.3 us; the launch traced here: 48.9 us
  Pallas kernels  48.3 us (98%)
  between operations  0.64 us (1%)
    pallas_call x1, Pallas kernels, on_device(): pl.pallas_call(functools.partial(kernel, sizes, unroll), out_shape=(jax.S...  47 us
    pallas_call x1, Pallas kernels, on_device(): pl.pallas_call(finish, out_shape=tuple((jax.ShapeDtypeStruct(r.shape, f32...  1.33 us

profile of v4, /device:TPU:0, one launch (start us, length us, event | category | flops | bytes accessed | tf_op | source)
XLA Modules:
  0.0 48.9 jit_solution(17793073075817757881)
XLA Ops:
  0.6 47.0 %shard_map.76 = (f32[3,8,128]{2,1,0:T(8,128)}, f32[3,8,128]{2,1,0:T(8,128)}, f32[2,3]{1,0:T(2,128)}) custom-call(f32[3,8,128]{2,1,0:T(8,128)} %pos_hbm.1, f32[3,8,128]{2,1,0:T(8,128)} %vel_hbm.1, s32[178]{0:T(256)} %send_hbm.1, s32[2,1792]{1,0:T(2,128)} %pair_hbm.1, s32[7,128]{1,0:T(8,128)} %flag_hbm.1), custom_call_target="tpu_custom_call" | custom-call | tf_op jit(solution)/shard_map/pallas_call | solution.py:492
  47.6 1.3 %shard_map.77 = (f32[3,8,128]{2,1,0:T(8,128)}, f32[3,8,128]{2,1,0:T(8,128)}, f32[2,3]{1,0:T(2,128)}) custom-call(f32[3,8,128]{2,1,0:T(8,128)} %get-tuple-element.9.coords, f32[3,8,128]{2,1,0:T(8,128)} %get-tuple-element.10.speeds, f32[2,3]{1,0:T(2,128)} %get-tuple-element.11.sums), custom_call_target="tpu_custom_call" | custom-call | tf_op jit(solution)/shard_map/pallas_call | solution.py:537
